TPU v7x, 32 devices: a whole 2x2x4 slice. The times are simulated.
32 devices in a mesh: replica: 2 (over y), expert: 8 (over z, core), tensor: 2 (over x).
Axes of the slice: x: 2, y: 2, z: 4, core: 2. Of those that a mesh axis runs over, the one named last changes fastest.
Arguments:
- delta: bfloat16 [2, 128, 4, 14336], P('replica', 'expert', None, 'tensor'), may hold values from -6 to 6
- step_offsets: int32 [2], replicated, may hold values from 0 to 15, as said below
- block_map: int32 [128], replicated, may hold values from 0 to 127, as said below
- master_params: float32 [128, 4, 14336], P('expert', 'replica', 'tensor'), may hold values from -6 to 6
- first_moment: float32 [128, 4, 14336], P('expert', 'replica', 'tensor'), may hold values from -2 to 2
- second_moment: float32 [128, 4, 14336], P('expert', 'replica', 'tensor'), may hold values from 0.01 to 1
Outputs:
- new_params: bfloat16 [128, 4, 14336], P('expert', 'replica')
- new_first: float32 [128, 4, 14336], P('expert', 'replica', 'tensor')
- new_second: float32 [128, 4, 14336], P('expert', 'replica', 'tensor')
Inputs may be any that keep to these rules, and one draw needn't show every extreme that they name: `block_map`: A permutation of the block indices onto owner slots; slot s belongs to expert index s // 16, and the blocks b with b // 16 = i go in equal numbers to every expert index. `step_offsets`: the replica groups' offsets are distinct.
All inputs are finite; a program needn't handle non-finite values.
Results may differ from a plain program's by a relative error of at most 0.0035.
Values may be sent and summed in bfloat16 or wider, within the bound.
A program may use at most 64 MiB of HBM per device.

v0:
```python
import functools

import jax
import jax.numpy as jnp
from jax import lax
from jax.experimental import pallas as pl
from jax.experimental.pallas import tpu as pltpu
from jax.sharding import PartitionSpec as P

beta_one = 0.9
beta_two = 0.99
outer_rate = 0.7
outer_round = 20
epsilon = 1e-08

LANES = 128
CHUNK = 8
LAG = 2
UNROLL = 16
MESH = pl.DeviceIdType.MESH


def kernel(
    sizes,
    block_map,
    step_offsets,
    delta,
    master_params,
    first_moment,
    second_moment,
    params,
    new_first,
    new_second,
    master,
    first,
    second,
    order,
    slots,
    places,
    load_sem,
    state_sem,
    own_sem,
    y_send,
    y_recv,
    z_send,
    z_recv,
    x_send,
    x_recv,
    *buffers,
):
    replicas, experts, tensors, chunks, blocks, pairs, rows = sizes
    count = len(chunks)
    stage = buffers[:count]
    arrived = buffers[count : 2 * count]
    outgoing = buffers[2 * count : 3 * count]
    incoming = buffers[3 * count :]
    my_replica = lax.axis_index("replica")
    my_expert = lax.axis_index("expert")
    my_tensor = lax.axis_index("tensor")
    columns = sum(chunks)
    starts = [sum(chunks[:c]) for c in range(count)]

    def load(c, d):
        replica = lax.rem(my_replica + d, replicas)
        return pltpu.make_async_copy(
            delta.at[:, pl.ds(starts[c], chunks[c]), replica],
            stage[c].at[d],
            load_sem.at[c, d],
        )

    def y_copy(c, d):
        return pltpu.make_async_remote_copy(
            src_ref=stage[c].at[d],
            dst_ref=arrived[c].at[d - 1],
            send_sem=y_send.at[c, d],
            recv_sem=y_recv.at[c, d],
            device_id={"replica": lax.rem(my_replica + d, replicas)},
            device_id_type=MESH,
        )

    def z_copy(c, d):
        peer = lax.rem(my_expert + d, experts)
        return pltpu.make_async_remote_copy(
            src_ref=outgoing[c].at[pl.ds(peer * pairs, pairs)],
            dst_ref=incoming[c].at[pl.ds(my_expert * pairs, pairs)],
            send_sem=z_send.at[c, d],
            recv_sem=z_recv.at[c, d],
            device_id={"expert": peer},
            device_id_type=MESH,
        )

    def z_own(c):
        mine = pl.ds(my_expert * pairs, pairs)
        return pltpu.make_async_copy(outgoing[c].at[mine], incoming[c].at[mine], own_sem.at[c])

    def x_copy(c, d):
        part = params.at[:, pl.ds(my_tensor * columns + starts[c], chunks[c])]
        return pltpu.make_async_remote_copy(
            src_ref=part,
            dst_ref=part,
            send_sem=x_send.at[c, d],
            recv_sem=x_recv.at[c, d],
            device_id={"tensor": lax.rem(my_tensor + d, tensors)},
            device_id_type=MESH,
        )

    barrier = pltpu.get_barrier_semaphore()
    axes = (("replica", my_replica, replicas), ("expert", my_expert, experts), ("tensor", my_tensor, tensors))
    for axis, mine, size in axes:
        for d in range(1, size):
            pl.semaphore_signal(
                barrier, inc=1, device_id={axis: lax.rem(mine + d, size)}, device_id_type=MESH
            )
    for c in range(count):
        for d in list(range(1, replicas)) + [0]:
            load(c, d).start()
    states = [
        pltpu.make_async_copy(source, held, state_sem.at[i])
        for i, (source, held) in enumerate(
            ((master_params, master), (first_moment, first), (second_moment, second))
        )
    ]
    for copy in states:
        copy.start()

    def note_order(e, carry):
        seen = jnp.int32(0)
        found = [jnp.int32(0)] * pairs
        for j in range(blocks):
            owned = lax.div(block_map[my_expert * blocks + j], jnp.int32(blocks)) == e
            for k in range(pairs):
                found[k] = jnp.where(owned, jnp.where(seen == k, j, found[k]), found[k])
            seen = seen + jnp.where(owned, 1, 0)
        for k in range(pairs):
            order[e * pairs + k] = found[k]
        return carry

    def note_slots(i, carry):
        seen = jnp.int32(0)
        found = [jnp.int32(0)] * pairs
        for j in range(blocks):
            slot = block_map[i * blocks + j] - my_expert * blocks
            owned = jnp.where(slot >= 0, jnp.where(slot < blocks, 1, 0), 0)
            for k in range(pairs):
                found[k] = jnp.where(owned == 1, jnp.where(seen == k, slot, found[k]), found[k])
            seen = seen + owned
        for k in range(pairs):
            slots[i * pairs + k] = found[k]
        return carry

    def note_places(s, carry):
        place = jnp.int32(0)
        for q in range(blocks):
            place = jnp.where(slots[q] == s, q, place)
        places[s] = place
        return carry

    lax.fori_loop(0, experts, note_order, 0)
    lax.fori_loop(0, experts, note_slots, 0)
    lax.fori_loop(0, blocks, note_places, 0)

    pl.semaphore_wait(barrier, replicas + experts + tensors - 3)
    for c in range(count):
        for d in range(1, replicas):
            load(c, d).wait()
            y_copy(c, d).start()

    shares = [
        1.0 / jnp.full((8, LANES), 1 + step_offsets[lax.rem(my_replica + replicas - d, replicas)], jnp.int32).astype(jnp.float32)
        for d in range(replicas)
    ]
    total = functools.reduce(lambda a, b: a + b, shares)
    weights = [(share / total)[:1] for share in shares]

    fix_one = 1.0 - beta_one**outer_round
    fix_two = 1.0 - beta_two**outer_round

    def add_up(c):
        load(c, 0).wait()
        for d in range(1, replicas):
            y_copy(c, d).wait_recv()
        dense = chunks[c] * rows
        own = stage[c].reshape(replicas, blocks, dense, LANES)
        others = arrived[c].reshape(replicas - 1, blocks, dense, LANES)
        out = outgoing[c].reshape(blocks, dense, LANES)

        def step(n, carry):
            for u in range(UNROLL):
                p = n * UNROLL + u
                block = order[p]
                value = own[0, block].astype(jnp.float32) * weights[0]
                for d in range(1, replicas):
                    value = value + others[d - 1, block].astype(jnp.float32) * weights[d]
                out[p] = value.astype(jnp.bfloat16)
            return carry

        lax.fori_loop(0, blocks // UNROLL, step, 0)

    def adam(c):
        dense = chunks[c] * rows
        terms = incoming[c].reshape(blocks, dense, LANES)
        held = params.reshape(blocks, tensors * columns * rows, LANES)
        part = pl.ds(starts[c] * rows, dense)
        target = pl.ds(pl.multiple_of((my_tensor * columns + starts[c]) * rows, 16), dense)

        def step(n, carry):
            for u in range(UNROLL):
                s = n * UNROLL + u
                gradient = terms[places[s]].astype(jnp.float32)
                one = beta_one * first[s, part] + (1.0 - beta_one) * gradient
                two = beta_two * second[s, part] + (1.0 - beta_two) * gradient * gradient
                new_first[s, part] = one
                new_second[s, part] = two
                update = (outer_rate / fix_one) * one / (jnp.sqrt(two * (1.0 / fix_two)) + epsilon)
                held[s, target] = (master[s, part] - update).astype(jnp.bfloat16)
            return carry

        lax.fori_loop(0, blocks // UNROLL, step, 0)

    def finish(c):
        if c == 0:
            for copy in states:
                copy.wait()
        z_own(c).wait()
        for d in range(1, experts):
            z_copy(c, d).wait_recv()
        adam(c)
        for d in range(1, tensors):
            x_copy(c, d).start()

    for c in range(count):
        add_up(c)
        for d in range(1, experts):
            z_copy(c, d).start()
        z_own(c).start()
        if c >= LAG:
            finish(c - LAG)
    for c in range(max(count - LAG, 0), count):
        finish(c)

    for c in range(count):
        for d in range(1, replicas):
            y_copy(c, d).wait_send()
        for d in range(1, experts):
            z_copy(c, d).wait_send()
    for c in range(count):
        for d in range(1, tensors):
            x_copy(c, d).wait()


def write_out(*refs):
    half = (len(refs) - 1) // 2
    sems = refs[-1]
    copies = [
        pltpu.make_async_copy(refs[i], refs[half + i], sems.at[i])
        for i in range(half)
    ]
    for copy in copies:
        copy.start()
    for copy in copies:
        copy.wait()


def body(delta, step_offsets, block_map, master_params, first_moment, second_moment, *, shape):
    replicas, experts, tensors = shape
    blocks, rows_all, width = delta.shape[1:]
    rows = rows_all // replicas
    columns = width // LANES
    pairs = blocks // experts
    chunks = [CHUNK] * (columns // CHUNK)
    count = len(chunks)
    terms = delta.reshape(blocks, replicas, rows, columns, LANES).transpose(0, 3, 1, 2, 4)

    def dense(state):
        split = state.reshape(blocks, rows, columns, LANES).transpose(0, 2, 1, 3)
        return split.reshape(blocks, columns * rows, LANES)

    def undense(state):
        split = state.reshape(blocks, columns, rows, LANES).transpose(0, 2, 1, 3)
        return split.reshape(blocks, rows, width)

    state_shape = (blocks, columns * rows, LANES)
    params_shape = (blocks, tensors * columns, rows, LANES)
    anywhere = pl.BlockSpec(memory_space=pltpu.HBM)
    near = pl.BlockSpec(memory_space=pltpu.VMEM)
    scalars = pl.BlockSpec(memory_space=pltpu.SMEM)
    dma = pltpu.SemaphoreType.DMA
    sizes = (replicas, experts, tensors, chunks, blocks, pairs, rows)
    held = pl.pallas_call(
        functools.partial(kernel, sizes),
        out_shape=(
            pltpu.VMEM(params_shape, jnp.bfloat16),
            pltpu.VMEM(state_shape, jnp.float32),
            pltpu.VMEM(state_shape, jnp.float32),
        ),
        in_specs=[scalars] * 2 + [anywhere] * 4,
        out_specs=(near,) * 3,
        scratch_shapes=[
            pltpu.VMEM(state_shape, jnp.float32),
            pltpu.VMEM(state_shape, jnp.float32),
            pltpu.VMEM(state_shape, jnp.float32),
            pltpu.SMEM((blocks,), jnp.int32),
            pltpu.SMEM((blocks,), jnp.int32),
            pltpu.SMEM((blocks,), jnp.int32),
            dma((count, replicas)),
            dma((3,)),
            dma((count,)),
            dma((count, replicas)),
            dma((count, replicas)),
            dma((count, experts)),
            dma((count, experts)),
            dma((count, tensors)),
            dma((count, tensors)),
        ]
        + [pltpu.VMEM((replicas, blocks, c, rows, LANES), jnp.bfloat16) for c in chunks]
        + [pltpu.VMEM((replicas - 1, blocks, c, rows, LANES), jnp.bfloat16) for c in chunks]
        + [pltpu.VMEM((blocks, c, rows, LANES), jnp.bfloat16) for c in chunks]
        + [pltpu.VMEM((blocks, c, rows, LANES), jnp.bfloat16) for c in chunks],
        compiler_params=pltpu.CompilerParams(collective_id=0, has_side_effects=True),
    )(block_map, step_offsets, terms, dense(master_params), dense(first_moment), dense(second_moment))
    new_params, new_first, new_second = pl.pallas_call(
        write_out,
        out_shape=(
            jax.ShapeDtypeStruct(params_shape, jnp.bfloat16),
            jax.ShapeDtypeStruct(state_shape, jnp.float32),
            jax.ShapeDtypeStruct(state_shape, jnp.float32),
        ),
        in_specs=[near] * 3,
        out_specs=(anywhere,) * 3,
        scratch_shapes=[dma((3,))],
        compiler_params=pltpu.CompilerParams(vmem_limit_bytes=1024 * 1024),
    )(*held)
    full = new_params.transpose(0, 2, 1, 3).reshape(blocks, rows, tensors * width)
    return (full, undense(new_first), undense(new_second))


def solution(mesh):
    in_specs = (
        P("replica", "expert", None, "tensor"),
        P(),
        P(),
        P("expert", "replica", "tensor"),
        P("expert", "replica", "tensor"),
        P("expert", "replica", "tensor"),
    )
    out_specs = (
        P("expert", "replica", None),
        P("expert", "replica", "tensor"),
        P("expert", "replica", "tensor"),
    )
    shape = tuple(mesh.shape[axis] for axis in ("replica", "expert", "tensor"))
    step = functools.partial(body, shape=shape)
    return jax.shard_map(step, mesh=mesh, in_specs=in_specs, out_specs=out_specs, check_vma=False)
```

profile of v0, /device:TPU:0, one launch (start us, length us, event | category | flops | bytes accessed | tf_op | source)
XLA Modules:
  0.0 30.8 jit_solution(13070434902727717776)
XLA Ops:
  0.6 28.6 %shard_map.85 = (bf16[16,112,2,128]{3,2,1,0:T(2,128)(2,1)S(1)}, f32[16,112,128]{2,1,0:T(8,128)S(1)}, f32[16,112,128]{2,1,0:T(8,128)S(1)}) custom-call(s32[128]{0:T(128)} %block_map.1, s32[2]{0:T(128)} %step_offsets.1, bf16[16,56,2,2,128]{4,3,2,1,0:T(2,128)(2,1)} %bitcast.31, f32[16,112,128]{2,1,0:T(8,128)} %bitcast.32, f32[16,112,128]{2,1,0:T(8,128)} %bitcast.33, ...), custom_call_target="tpu_custom_call" | custom-call | tf_op jit(solution)/shard_map/pallas_call | solution.py:289
  29.2 1.6 %shard_map.86 = (bf16[16,112,2,128]{3,2,1,0:T(2,128)(2,1)}, f32[16,112,128]{2,1,0:T(8,128)}, f32[16,112,128]{2,1,0:T(8,128)}) custom-call(bf16[16,112,2,128]{3,2,1,0:T(2,128)(2,1)S(1)} %get-tuple-element.9.refs_0_, f32[16,112,128]{2,1,0:T(8,128)S(1)} %get-tuple-element.10.refs_1_, f32[16,112,128]{2,1,0:T(8,128)S(1)} %get-tuple-element.11.refs_2_), custom_call_target="tpu_custom_call" | custom-call | tf_op jit(solution)/shard_map/pallas_call | solution.py:321
where the time goes:
time: 30.9 us; the launch traced here: 30.8 us
  Pallas kernels  30.1 us (97%)
  between operations  0.64 us (2%)
    pallas_call x1, Pallas kernels, body(): pl.pallas_call(functools.partial(kernel, sizes), out_shape=(pltpu.VMEM(pa...  28.6 us
    pallas_call x1, Pallas kernels, body(): pl.pallas_call(write_out, out_shape=(jax.ShapeDtypeStruct(params_shape, j...  1.56 us

commit v1 on v0

--- a/solution.py
+++ b/solution.py
@@ -15,15 +15,28 @@
 
 LANES = 128
 CHUNK = 8
+EDGE = 4
 LAG = 2
 UNROLL = 16
 MESH = pl.DeviceIdType.MESH
 
 
+def flipped(mine, d, size):
+    if size & (size - 1):
+        return lax.rem(mine + d, size)
+    peer = mine
+    bit = 1
+    while bit < size:
+        if d & bit:
+            peer = peer + bit * (1 - 2 * lax.rem(lax.div(mine, bit), 2))
+        bit *= 2
+    return peer
+
+
 def kernel(
     sizes,
-    block_map,
-    step_offsets,
+    block_map_far,
+    step_offsets_far,
     delta,
     master_params,
     first_moment,
@@ -34,12 +47,14 @@
     master,
     first,
     second,
+    block_map,
+    step_offsets,
     order,
     slots,
     places,
+    index_sem,
     load_sem,
     state_sem,
-    own_sem,
     y_send,
     y_recv,
     z_send,
@@ -72,48 +87,55 @@
         return pltpu.make_async_remote_copy(
             src_ref=stage[c].at[d],
             dst_ref=arrived[c].at[d - 1],
-            send_sem=y_send.at[c, d],
-            recv_sem=y_recv.at[c, d],
+            send_sem=y_send,
+            recv_sem=y_recv.at[c],
             device_id={"replica": lax.rem(my_replica + d, replicas)},
             device_id_type=MESH,
         )
 
     def z_copy(c, d):
-        peer = lax.rem(my_expert + d, experts)
+        peer = flipped(my_expert, d, experts)
         return pltpu.make_async_remote_copy(
             src_ref=outgoing[c].at[pl.ds(peer * pairs, pairs)],
             dst_ref=incoming[c].at[pl.ds(my_expert * pairs, pairs)],
-            send_sem=z_send.at[c, d],
-            recv_sem=z_recv.at[c, d],
+            send_sem=z_send,
+            recv_sem=z_recv.at[c],
             device_id={"expert": peer},
             device_id_type=MESH,
         )
-
-    def z_own(c):
-        mine = pl.ds(my_expert * pairs, pairs)
-        return pltpu.make_async_copy(outgoing[c].at[mine], incoming[c].at[mine], own_sem.at[c])
 
     def x_copy(c, d):
         part = params.at[:, pl.ds(my_tensor * columns + starts[c], chunks[c])]
         return pltpu.make_async_remote_copy(
             src_ref=part,
             dst_ref=part,
-            send_sem=x_send.at[c, d],
-            recv_sem=x_recv.at[c, d],
+            send_sem=x_send,
+            recv_sem=x_recv,
             device_id={"tensor": lax.rem(my_tensor + d, tensors)},
             device_id_type=MESH,
         )
 
+    def all_of(ref, sem):
+        return pltpu.make_async_copy(ref, ref, sem)
+
     barrier = pltpu.get_barrier_semaphore()
-    axes = (("replica", my_replica, replicas), ("expert", my_expert, experts), ("tensor", my_tensor, tensors))
+    axes = (("expert", my_expert, experts), ("replica", my_replica, replicas), ("tensor", my_tensor, tensors))
     for axis, mine, size in axes:
-        for d in range(1, size):
+        for d in reversed(range(1, size)):
             pl.semaphore_signal(
                 barrier, inc=1, device_id={axis: lax.rem(mine + d, size)}, device_id_type=MESH
             )
     for c in range(count):
-        for d in list(range(1, replicas)) + [0]:
+        for d in range(1, replicas):
             load(c, d).start()
+    index_copies = [
+        pltpu.make_async_copy(block_map_far, block_map, index_sem.at[0]),
+        pltpu.make_async_copy(step_offsets_far, step_offsets, index_sem.at[1]),
+    ]
+    for copy in index_copies:
+        copy.start()
+    for c in range(count):
+        load(c, 0).start()
     states = [
         pltpu.make_async_copy(source, held, state_sem.at[i])
         for i, (source, held) in enumerate(
@@ -155,15 +177,17 @@
         places[s] = place
         return carry
 
+    pl.semaphore_wait(barrier, replicas + experts + tensors - 3)
+    for c in range(count):
+        for d in range(1, replicas):
+            load(c, d).wait()
+            y_copy(c, d).start()
+
+    for copy in index_copies:
+        copy.wait()
     lax.fori_loop(0, experts, note_order, 0)
     lax.fori_loop(0, experts, note_slots, 0)
     lax.fori_loop(0, blocks, note_places, 0)
-
-    pl.semaphore_wait(barrier, replicas + experts + tensors - 3)
-    for c in range(count):
-        for d in range(1, replicas):
-            load(c, d).wait()
-            y_copy(c, d).start()
 
     shares = [
         1.0 / jnp.full((8, LANES), 1 + step_offsets[lax.rem(my_replica + replicas - d, replicas)], jnp.int32).astype(jnp.float32)
@@ -177,8 +201,7 @@
 
     def add_up(c):
         load(c, 0).wait()
-        for d in range(1, replicas):
-            y_copy(c, d).wait_recv()
+        all_of(arrived[c], y_recv.at[c]).wait()
         dense = chunks[c] * rows
         own = stage[c].reshape(replicas, blocks, dense, LANES)
         others = arrived[c].reshape(replicas - 1, blocks, dense, LANES)
@@ -201,7 +224,7 @@
         terms = incoming[c].reshape(blocks, dense, LANES)
         held = params.reshape(blocks, tensors * columns * rows, LANES)
         part = pl.ds(starts[c] * rows, dense)
-        target = pl.ds(pl.multiple_of((my_tensor * columns + starts[c]) * rows, 16), dense)
+        target = pl.ds(pl.multiple_of((my_tensor * columns + starts[c]) * rows, 8), dense)
 
         def step(n, carry):
             for u in range(UNROLL):
@@ -221,31 +244,28 @@
         if c == 0:
             for copy in states:
                 copy.wait()
-        z_own(c).wait()
-        for d in range(1, experts):
-            z_copy(c, d).wait_recv()
+        all_of(incoming[c].at[pl.ds(0, (experts - 1) * pairs)], z_recv.at[c]).wait()
+        mine = pl.ds(my_expert * pairs, pairs)
+        incoming[c][mine] = outgoing[c][mine]
         adam(c)
         for d in range(1, tensors):
             x_copy(c, d).start()
 
     for c in range(count):
         add_up(c)
-        for d in range(1, experts):
+        for d in reversed(range(1, experts)):
             z_copy(c, d).start()
-        z_own(c).start()
         if c >= LAG:
             finish(c - LAG)
     for c in range(max(count - LAG, 0), count):
         finish(c)
 
     for c in range(count):
-        for d in range(1, replicas):
-            y_copy(c, d).wait_send()
-        for d in range(1, experts):
-            z_copy(c, d).wait_send()
-    for c in range(count):
-        for d in range(1, tensors):
-            x_copy(c, d).wait()
+        all_of(arrived[c], y_send).wait()
+        all_of(incoming[c].at[pl.ds(0, (experts - 1) * pairs)], z_send).wait()
+    others = params.at[:, pl.ds(0, (tensors - 1) * columns)]
+    all_of(others, x_send).wait()
+    all_of(others, x_recv).wait()
 
 
 def write_out(*refs):
@@ -261,13 +281,18 @@
         copy.wait()
 
 
+def split(columns):
+    middle = columns - 2 * EDGE
+    return [EDGE] + [CHUNK] * (middle // CHUNK) + [EDGE]
+
+
 def body(delta, step_offsets, block_map, master_params, first_moment, second_moment, *, shape):
     replicas, experts, tensors = shape
     blocks, rows_all, width = delta.shape[1:]
     rows = rows_all // replicas
     columns = width // LANES
     pairs = blocks // experts
-    chunks = [CHUNK] * (columns // CHUNK)
+    chunks = split(columns)
     count = len(chunks)
     terms = delta.reshape(blocks, replicas, rows, columns, LANES).transpose(0, 3, 1, 2, 4)
 
@@ -283,7 +308,6 @@
     params_shape = (blocks, tensors * columns, rows, LANES)
     anywhere = pl.BlockSpec(memory_space=pltpu.HBM)
     near = pl.BlockSpec(memory_space=pltpu.VMEM)
-    scalars = pl.BlockSpec(memory_space=pltpu.SMEM)
     dma = pltpu.SemaphoreType.DMA
     sizes = (replicas, experts, tensors, chunks, blocks, pairs, rows)
     held = pl.pallas_call(
@@ -293,24 +317,26 @@
             pltpu.VMEM(state_shape, jnp.float32),
             pltpu.VMEM(state_shape, jnp.float32),
         ),
-        in_specs=[scalars] * 2 + [anywhere] * 4,
+        in_specs=[anywhere] * 6,
         out_specs=(near,) * 3,
         scratch_shapes=[
             pltpu.VMEM(state_shape, jnp.float32),
             pltpu.VMEM(state_shape, jnp.float32),
             pltpu.VMEM(state_shape, jnp.float32),
+            pltpu.SMEM(block_map.shape, jnp.int32),
+            pltpu.SMEM(step_offsets.shape, jnp.int32),
             pltpu.SMEM((blocks,), jnp.int32),
             pltpu.SMEM((blocks,), jnp.int32),
             pltpu.SMEM((blocks,), jnp.int32),
+            dma((2,)),
             dma((count, replicas)),
             dma((3,)),
+            dma,
             dma((count,)),
-            dma((count, replicas)),
-            dma((count, replicas)),
-            dma((count, experts)),
-            dma((count, experts)),
-            dma((count, tensors)),
-            dma((count, tensors)),
+            dma,
+            dma((count,)),
+            dma,
+            dma,
         ]
         + [pltpu.VMEM((replicas, blocks, c, rows, LANES), jnp.bfloat16) for c in chunks]
         + [pltpu.VMEM((replicas - 1, blocks, c, rows, LANES), jnp.bfloat16) for c in chunks]

time: 30.9 us -> 28.6 us (0.926)
  Pallas kernels: 30.1 us -> 27.8 us
    pallas_call x1, Pallas kernels: 28.6 us -> 26.2 us  [body(): pl.pallas_call(functools.partial(kernel, sizes), out_shape=(pltpu.VMEM(pa...]
where the time goes in v1:
time: 28.6 us; the launch traced here: 28.4 us
  Pallas kernels  27.8 us (97%)
  between operations  0.64 us (2%)
    pallas_call x1, Pallas kernels, body(): pl.pallas_call(functools.partial(kernel, sizes), out_shape=(pltpu.VMEM(pa...  26.2 us
    pallas_call x1, Pallas kernels, body(): pl.pallas_call(write_out, out_shape=(jax.ShapeDtypeStruct(params_shape, j...  1.56 us

profile of v1, /device:TPU:0, one launch (start us, length us, event | category | flops | bytes accessed | tf_op | source)
XLA Modules:
  0.0 28.4 jit_solution(928735872268130439)
XLA Ops:
  0.6 26.2 %shard_map.85 = (bf16[16,112,2,128]{3,2,1,0:T(2,128)(2,1)S(1)}, f32[16,112,128]{2,1,0:T(8,128)S(1)}, f32[16,112,128]{2,1,0:T(8,128)S(1)}) custom-call(s32[128]{0:T(128)} %block_map_far.1, s32[2]{0:T(128)} %step_offsets_far.1, bf16[16,56,2,2,128]{4,3,2,1,0:T(2,128)(2,1)} %bitcast.31, f32[16,112,128]{2,1,0:T(8,128)} %bitcast.32, f32[16,112,128]{2,1,0:T(8,128)} %bitcast.33, ...), custom_call_target="tpu_custom_call" | custom-call | tf_op jit(solution)/shard_map/pallas_call | solution.py:313
  26.9 1.6 %shard_map.86 = (bf16[16,112,2,128]{3,2,1,0:T(2,128)(2,1)}, f32[16,112,128]{2,1,0:T(8,128)}, f32[16,112,128]{2,1,0:T(8,128)}) custom-call(bf16[16,112,2,128]{3,2,1,0:T(2,128)(2,1)S(1)} %get-tuple-element.9.refs_0_, f32[16,112,128]{2,1,0:T(8,128)S(1)} %get-tuple-element.10.refs_1_, f32[16,112,128]{2,1,0:T(8,128)S(1)} %get-tuple-element.11.refs_2_), custom_call_target="tpu_custom_call" | custom-call | tf_op jit(solution)/shard_map/pallas_call | solution.py:347

commit v2 on v1

v2 whole, which is shorter than its diff:
```python
import functools

import jax
import jax.numpy as jnp
from jax import lax
from jax.experimental import pallas as pl
from jax.experimental.pallas import tpu as pltpu
from jax.sharding import PartitionSpec as P

beta_one = 0.9
beta_two = 0.99
outer_rate = 0.7
outer_round = 20
epsilon = 1e-08

LANES = 128
CHUNK = 4
EDGE = 4
LATE = 8
TURN = 21
EARLY = 99
LAGS = (8, 16, 24)
MESH = pl.DeviceIdType.MESH


def target(mine, d, size):
    if size & (size - 1):
        return lax.rem(mine + d, size)
    if not isinstance(d, int):
        peer = mine
        bit = 1
        while bit < size:
            both = lax.rem(lax.div(mine, bit), 2) * lax.rem(lax.div(d, bit), 2)
            peer = peer + bit * (lax.rem(lax.div(d, bit), 2) - 2 * both)
            bit *= 2
        return peer
    peer = mine
    bit = 1
    while bit < size:
        if d & bit:
            peer = peer + bit * (1 - 2 * lax.rem(lax.div(mine, bit), 2))
        bit *= 2
    return peer


def origin(mine, d, size):
    if size & (size - 1):
        return lax.rem(mine + size - d, size)
    return target(mine, d, size)


def kernel(
    sizes,
    block_map_far,
    step_offsets_far,
    delta,
    master_params,
    first_moment,
    second_moment,
    params,
    new_first,
    new_second,
    state,
    first_held,
    second_held,
    own,
    params_held,
    params_arrived,
    block_map,
    step_offsets,
    order,
    slots,
    places,
    index_sem,
    load_sem,
    own_sem,
    state_sem,
    y_send,
    y_recv,
    z_send,
    z_recv,
    late_recv,
    x_send,
    x_recv,
    *buffers,
):
    replicas, experts, tensors, chunks, late, blocks, pairs, rows = sizes
    count = len(chunks)
    stage = buffers[: count + 1]
    arrived = buffers[count + 1 : 2 * count + 1]
    outgoing = buffers[2 * count + 1 : 3 * count + 1]
    incoming = buffers[3 * count + 1 : 4 * count + 1]
    late_out, late_in, late_arrived = buffers[4 * count + 1 :]
    my_replica = lax.axis_index("replica")
    my_expert = lax.axis_index("expert")
    my_tensor = lax.axis_index("tensor")
    widths = chunks + [late]
    columns = sum(widths)
    starts = [sum(widths[:c]) for c in range(count + 1)]
    groups = [(0, 2), (2, 4), (4, experts)]

    def load(c, d):
        replica = lax.rem(my_replica + d, replicas)
        return pltpu.make_async_copy(
            delta.at[:, pl.ds(starts[c], widths[c]), replica],
            stage[c].at[d - 1],
            load_sem.at[c, d - 1],
        )

    def y_copy(c, d):
        return pltpu.make_async_remote_copy(
            src_ref=late_in.at[:, d] if c == count else stage[c].at[d - 1],
            dst_ref=late_arrived.at[d - 1] if c == count else arrived[c].at[d - 1],
            send_sem=y_send,
            recv_sem=y_recv.at[c],
            device_id={"replica": lax.rem(my_replica + d, replicas)},
            device_id_type=MESH,
        )

    def z_copy(c, d):
        part = pl.ds(d * pairs, pairs)
        return pltpu.make_async_remote_copy(
            src_ref=late_out.at[d] if c == count else outgoing[c].at[part],
            dst_ref=late_in.at[d] if c == count else incoming[c].at[part],
            send_sem=z_send,
            recv_sem=late_recv if c == count else z_recv.at[c, group_of(d)],
            device_id={"expert": target(my_expert, d, experts)},
            device_id_type=MESH,
        )

    def group_of(d):
        return [g for g, (low, high) in enumerate(groups) if low <= d < high][0]

    def x_copy(c, low, high, d):
        part = (pl.ds(low * pairs, (high - low) * pairs), pl.ds(starts[c], widths[c]))
        return pltpu.make_async_remote_copy(
            src_ref=params_held.at[part],
            dst_ref=params_arrived.at[(d - 1,) + part],
            send_sem=x_send,
            recv_sem=x_recv,
            device_id={"tensor": lax.rem(my_tensor + d, tensors)},
            device_id_type=MESH,
        )

    def all_of(ref, sem):
        return pltpu.make_async_copy(ref, ref, sem)

    barrier = pltpu.get_barrier_semaphore()
    axes = (("expert", my_expert, experts), ("replica", my_replica, replicas), ("tensor", my_tensor, tensors))
    for axis, mine, size in axes:
        for d in reversed(range(1, size)):
            pl.semaphore_signal(
                barrier, inc=1, device_id={axis: lax.rem(mine + d, size)}, device_id_type=MESH
            )
    for c in range(count + 1):
        for d in range(1, replicas):
            load(c, d).start()
    index_copies = [
        pltpu.make_async_copy(block_map_far, block_map, index_sem.at[0]),
        pltpu.make_async_copy(step_offsets_far, step_offsets, index_sem.at[1]),
    ]
    for copy in index_copies:
        copy.start()
    own_load = pltpu.make_async_copy(delta.at[:, :, my_replica], own, own_sem)
    own_load.start()
    for i, source in enumerate((master_params, first_moment, second_moment)):
        pltpu.make_async_copy(source, state.at[i], state_sem).start()

    def digits(key, k):
        return jnp.maximum(lax.rem(lax.div(key, jnp.int32(blocks ** (pairs - 1 - k))), jnp.int32(blocks)), 0)

    def note_order(d, carry):
        low = target(my_expert, d, experts) * blocks
        key = jnp.int32(0)
        for j in range(blocks):
            slot = block_map[my_expert * blocks + j] - low
            owned = jnp.where(slot >= 0, slot, blocks) < blocks
            key = jnp.where(owned, key * blocks + j, key)
        for k in range(pairs):
            order[d * pairs + k] = digits(key, k)
        return carry

    def note_slots(d, carry):
        low = origin(my_expert, d, experts) * blocks
        key = jnp.int32(0)
        for j in range(blocks):
            slot = block_map[low + j] - my_expert * blocks
            owned = jnp.where(slot >= 0, slot, blocks) < blocks
            key = jnp.where(owned, key * blocks + slot, key)
        for k in range(pairs):
            slots[d * pairs + k] = digits(key, k)
        return carry

    def note_places(s, carry):
        place = jnp.int32(0)
        for q in range(blocks):
            place = jnp.where(slots[q] == s, q, place)
        places[s] = place
        return carry

    pl.semaphore_wait(barrier, replicas + experts + tensors - 3)
    early = min(EARLY, count)
    for c in range(early):
        for d in range(1, replicas):
            load(c, d).wait()
            y_copy(c, d).start()

    for copy in index_copies:
        copy.wait()
    lax.fori_loop(0, experts, note_order, 0)

    own_load.wait()
    for c in range(early, count + 1):
        for d in range(1, replicas):
            load(c, d).wait()
    late_dense = late * rows
    for d in range(experts):
        held = (late_in if d == 0 else late_out).reshape(experts, replicas, pairs, late_dense, LANES)
        own_flat = own.reshape(blocks, columns * rows, LANES)
        rest = stage[count].reshape(replicas - 1, blocks, late_dense, LANES)
        for k in range(pairs):
            block = order[d * pairs + k]
            held[d, 0, k] = own_flat[block, pl.ds(starts[count] * rows, late_dense)]
            for r in range(1, replicas):
                held[d, r, k] = rest[r - 1, block]
    for d in reversed(range(1, experts)):
        z_copy(count, d).start()

    lax.fori_loop(0, experts, note_slots, 0)
    lax.fori_loop(0, blocks, note_places, 0)

    shares = [
        1.0 / jnp.full((8, LANES), 1 + step_offsets[lax.rem(my_replica + replicas - d, replicas)], jnp.int32).astype(jnp.float32)
        for d in range(replicas)
    ]
    total = functools.reduce(lambda a, b: a + b, shares)
    weights = [(share / total)[:1] for share in shares]

    fix_one = 1.0 - beta_one**outer_round
    fix_two = 1.0 - beta_two**outer_round

    def add_up(c):
        all_of(arrived[c], y_recv.at[c]).wait()
        dense = chunks[c] * rows
        part = pl.ds(starts[c] * rows, dense)
        own_flat = own.reshape(blocks, columns * rows, LANES)
        others = arrived[c].reshape(replicas - 1, blocks, dense, LANES)
        out = outgoing[c].reshape(blocks, dense, LANES)
        for q in range(blocks):
            block = order[q]
            value = own_flat[block, part].astype(jnp.float32) * weights[0]
            for d in range(1, replicas):
                value = value + others[d - 1, block].astype(jnp.float32) * weights[d]
            out[q] = value.astype(jnp.bfloat16)

    def adam(c, q, gradient):
        part = pl.ds(starts[c] * rows, widths[c] * rows)
        slot = slots[q]
        one = beta_one * state[1, slot, part] + (1.0 - beta_one) * gradient
        two = beta_two * state[2, slot, part] + (1.0 - beta_two) * gradient * gradient
        first_held[q, part] = one
        second_held[q, part] = two
        update = (outer_rate / fix_one) * one / (jnp.sqrt(two * (1.0 / fix_two)) + epsilon)
        held = params_held.reshape(blocks, columns * rows, LANES)
        held[q, part] = (state[0, slot, part] - update).astype(jnp.bfloat16)

    def finish(c, g):
        if c == 0 and g == 0:
            all_of(state, state_sem).wait()
        low, high = groups[g]
        got = (max(low, 1) * pairs, high * pairs)
        all_of(incoming[c].at[pl.ds(got[0], got[1] - got[0])], z_recv.at[c, g]).wait()
        dense = chunks[c] * rows
        for q in range(low * pairs, high * pairs):
            terms = (outgoing[c] if q < pairs else incoming[c]).reshape(blocks, dense, LANES)
            adam(c, q, terms[q].astype(jnp.float32))
        for d in range(1, tensors):
            x_copy(c, low, high, d).start()

    def finish_late():
        all_of(late_arrived, y_recv.at[count]).wait()
        mine = late_in.reshape(experts, replicas, pairs, late_dense, LANES)
        others = late_arrived.reshape(replicas - 1, experts, pairs, late_dense, LANES)
        for q in range(blocks):
            e, k = divmod(q, pairs)
            value = mine[e, 0, k].astype(jnp.float32) * weights[0]
            for d in range(1, replicas):
                value = value + others[d - 1, e, k].astype(jnp.float32) * weights[d]
            adam(count, q, value)
        for d in range(1, tensors):
            x_copy(count, 0, experts, d).start()

    def settle(c):
        part = pl.ds(starts[c] * rows, widths[c] * rows)
        goal = pl.ds(pl.multiple_of((my_tensor * columns + starts[c]) * rows, 8), widths[c] * rows)
        flat = params.reshape(blocks, tensors * columns * rows, LANES)
        held = params_held.reshape(blocks, columns * rows, LANES)
        for s in range(blocks):
            place = places[s]
            new_first[s, part] = first_held[place, part]
            new_second[s, part] = second_held[place, part]
            flat[s, goal] = held[place, part]

    def add_and_send(c):
        add_up(c)
        for d in reversed(range(1, experts)):
            z_copy(c, d).start()

    def turn():
        all_of(late_in.at[pl.ds(1, experts - 1)], late_recv).wait()
        for c in [count] + list(range(early, count)):
            for d in range(1, replicas):
                y_copy(c, d).start()

    def last(c):
        finish(c, 2)
        settle(c)

    def whole_late():
        finish_late()
        settle(count)

    steps = [(TURN, 0, turn)]
    landed = 0
    for c in list(range(early)) + [count] + list(range(early, count)):
        landed += widths[c]
        if c == count:
            steps.append((landed, 2, whole_late))
            continue
        steps.append((landed, 1, functools.partial(add_and_send, c)))
        steps.append((landed + LAGS[0], 3, functools.partial(finish, c, 0)))
        steps.append((landed + LAGS[1], 4, functools.partial(finish, c, 1)))
        steps.append((landed + LAGS[2], 5, functools.partial(last, c)))
    for _, _, step in sorted(steps, key=lambda entry: entry[:2]):
        step()

    for c in range(count):
        all_of(arrived[c], y_send).wait()
        all_of(incoming[c].at[pl.ds(0, (experts - 1) * pairs)], z_send).wait()
    all_of(late_arrived, y_send).wait()
    all_of(late_in.at[pl.ds(1, experts - 1)], z_send).wait()
    all_of(params_arrived, x_send).wait()
    all_of(params_arrived, x_recv).wait()
    flat = params.reshape(blocks, tensors * columns * rows, LANES)
    others = params_arrived.reshape(tensors - 1, blocks, columns * rows, LANES)
    for d in range(1, tensors):
        sender = lax.rem(my_tensor + tensors - d, tensors)
        goal = pl.ds(pl.multiple_of(sender * columns * rows, 8), columns * rows)
        for s in range(blocks):
            flat[s, goal] = others[d - 1, places[s]]


def write_out(*refs):
    half = (len(refs) - 1) // 2
    sems = refs[-1]
    copies = [
        pltpu.make_async_copy(refs[i], refs[half + i], sems.at[i])
        for i in range(half)
    ]
    for copy in copies:
        copy.start()
    for copy in copies:
        copy.wait()


def split(columns):
    late = LATE
    middle = columns - late - 2 * EDGE
    return [EDGE] + [CHUNK] * (middle // CHUNK) + [EDGE] * (1 + middle % CHUNK // EDGE), late


def body(delta, step_offsets, block_map, master_params, first_moment, second_moment, *, shape):
    replicas, experts, tensors = shape
    blocks, rows_all, width = delta.shape[1:]
    rows = rows_all // replicas
    columns = width // LANES
    pairs = blocks // experts
    chunks, late = split(columns)
    count = len(chunks)
    terms = delta.reshape(blocks, replicas, rows, columns, LANES).transpose(0, 3, 1, 2, 4)

    def dense(state):
        split = state.reshape(blocks, rows, columns, LANES).transpose(0, 2, 1, 3)
        return split.reshape(blocks, columns * rows, LANES)

    def undense(state):
        split = state.reshape(blocks, columns, rows, LANES).transpose(0, 2, 1, 3)
        return split.reshape(blocks, rows, width)

    state_shape = (blocks, columns * rows, LANES)
    params_shape = (blocks, tensors * columns, rows, LANES)
    anywhere = pl.BlockSpec(memory_space=pltpu.HBM)
    near = pl.BlockSpec(memory_space=pltpu.VMEM)
    dma = pltpu.SemaphoreType.DMA
    sizes = (replicas, experts, tensors, chunks, late, blocks, pairs, rows)
    piece = (rows, LANES)
    held = pl.pallas_call(
        functools.partial(kernel, sizes),
        out_shape=(
            pltpu.VMEM(params_shape, jnp.bfloat16),
            pltpu.VMEM(state_shape, jnp.float32),
            pltpu.VMEM(state_shape, jnp.float32),
        ),
        in_specs=[anywhere] * 6,
        out_specs=(near,) * 3,
        scratch_shapes=[
            pltpu.VMEM((3,) + state_shape, jnp.float32),
            pltpu.VMEM(state_shape, jnp.float32),
            pltpu.VMEM(state_shape, jnp.float32),
            pltpu.VMEM((blocks, columns) + piece, jnp.bfloat16),
            pltpu.VMEM((blocks, columns) + piece, jnp.bfloat16),
            pltpu.VMEM((tensors - 1, blocks, columns) + piece, jnp.bfloat16),
            pltpu.SMEM(block_map.shape, jnp.int32),
            pltpu.SMEM(step_offsets.shape, jnp.int32),
            pltpu.SMEM((blocks,), jnp.int32),
            pltpu.SMEM((blocks,), jnp.int32),
            pltpu.SMEM((blocks,), jnp.int32),
            dma((2,)),
            dma((count + 1, replicas - 1)),
            dma,
            dma,
            dma,
            dma((count + 1,)),
            dma,
            dma((count, 3)),
            dma,
            dma,
            dma,
        ]
        + [pltpu.VMEM((replicas - 1, blocks, c) + piece, jnp.bfloat16) for c in chunks + [late]]
        + [pltpu.VMEM((replicas - 1, blocks, c) + piece, jnp.bfloat16) for c in chunks]
        + [pltpu.VMEM((blocks, c) + piece, jnp.bfloat16) for c in chunks]
        + [pltpu.VMEM((blocks, c) + piece, jnp.bfloat16) for c in chunks]
        + [pltpu.VMEM((experts, replicas, pairs, late) + piece, jnp.bfloat16)] * 2
        + [pltpu.VMEM((replicas - 1, experts, pairs, late) + piece, jnp.bfloat16)],
        compiler_params=pltpu.CompilerParams(collective_id=0, has_side_effects=True),
    )(block_map, step_offsets, terms, dense(master_params), dense(first_moment), dense(second_moment))
    new_params, new_first, new_second = pl.pallas_call(
        write_out,
        out_shape=(
            jax.ShapeDtypeStruct(params_shape, jnp.bfloat16),
            jax.ShapeDtypeStruct(state_shape, jnp.float32),
            jax.ShapeDtypeStruct(state_shape, jnp.float32),
        ),
        in_specs=[near] * 3,
        out_specs=(anywhere,) * 3,
        scratch_shapes=[dma((3,))],
        compiler_params=pltpu.CompilerParams(vmem_limit_bytes=1024 * 1024),
    )(*held)
    full = new_params.transpose(0, 2, 1, 3).reshape(blocks, rows, tensors * width)
    return (full, undense(new_first), undense(new_second))


def solution(mesh):
    in_specs = (
        P("replica", "expert", None, "tensor"),
        P(),
        P(),
        P("expert", "replica", "tensor"),
        P("expert", "replica", "tensor"),
        P("expert", "replica", "tensor"),
    )
    out_specs = (
        P("expert", "replica", None),
        P("expert", "replica", "tensor"),
        P("expert", "replica", "tensor"),
    )
    shape = tuple(mesh.shape[axis] for axis in ("replica", "expert", "tensor"))
    step = functools.partial(body, shape=shape)
    return jax.shard_map(step, mesh=mesh, in_specs=in_specs, out_specs=out_specs, check_vma=False)
```

time: 28.6 us -> 27.5 us (0.962)
  Pallas kernels: 27.8 us -> 26.8 us
    pallas_call x1, Pallas kernels: 26.2 us -> 25.2 us  [body(): pl.pallas_call(functools.partial(kernel, sizes), out_shape=(pltpu.VMEM(pa...]
where the time goes in v2:
time: 27.5 us; the launch traced here: 27.4 us
  Pallas kernels  26.8 us (97%)
  between operations  0.64 us (2%)
    pallas_call x1, Pallas kernels, body(): pl.pallas_call(functools.partial(kernel, sizes), out_shape=(pltpu.VMEM(pa...  25.2 us
    pallas_call x1, Pallas kernels, body(): pl.pallas_call(write_out, out_shape=(jax.ShapeDtypeStruct(params_shape, j...  1.56 us

profile of v2, /device:TPU:0, one launch (start us, length us, event | category | flops | bytes accessed | tf_op | source)
XLA Modules:
  0.0 27.4 jit_solution(6155678044402506230)
XLA Ops:
  0.6 25.2 %shard_map.85 = (bf16[16,112,2,128]{3,2,1,0:T(2,128)(2,1)S(1)}, f32[16,112,128]{2,1,0:T(8,128)S(1)}, f32[16,112,128]{2,1,0:T(8,128)S(1)}) custom-call(s32[128]{0:T(128)} %block_map_far.1, s32[2]{0:T(128)} %step_offsets_far.1, bf16[16,56,2,2,128]{4,3,2,1,0:T(2,128)(2,1)} %bitcast.31, f32[16,112,128]{2,1,0:T(8,128)} %bitcast.32, f32[16,112,128]{2,1,0:T(8,128)} %bitcast.33, ...), custom_call_target="tpu_custom_call" | custom-call | tf_op jit(solution)/shard_map/pallas_call | solution.py:397
  25.8 1.6 %shard_map.86 = (bf16[16,112,2,128]{3,2,1,0:T(2,128)(2,1)}, f32[16,112,128]{2,1,0:T(8,128)}, f32[16,112,128]{2,1,0:T(8,128)}) custom-call(bf16[16,112,2,128]{3,2,1,0:T(2,128)(2,1)S(1)} %get-tuple-element.9.refs_0_, f32[16,112,128]{2,1,0:T(8,128)S(1)} %get-tuple-element.10.refs_1_, f32[16,112,128]{2,1,0:T(8,128)S(1)} %get-tuple-element.11.refs_2_), custom_call_target="tpu_custom_call" | custom-call | tf_op jit(solution)/shard_map/pallas_call | solution.py:438

commit v3 on v2

--- a/solution.py
+++ b/solution.py
@@ -17,9 +17,12 @@
 CHUNK = 4
 EDGE = 4
 LATE = 8
+SORTS = (4, 4)
+REST = (11, 13)
+AHEAD = 7
 TURN = 21
-EARLY = 99
 LAGS = (8, 16, 24)
+FIRST_LAGS = (8, 16, 24)
 MESH = pl.DeviceIdType.MESH
 
 
@@ -41,6 +44,12 @@
             peer = peer + bit * (1 - 2 * lax.rem(lax.div(mine, bit), 2))
         bit *= 2
     return peer
+
+
+def between(mine, peer, size):
+    if size & (size - 1):
+        return lax.rem(peer + size - mine, size)
+    return target(mine, peer, size)
 
 
 def origin(mine, d, size):
@@ -84,35 +93,51 @@
     x_recv,
     *buffers,
 ):
-    replicas, experts, tensors, chunks, late, blocks, pairs, rows = sizes
-    count = len(chunks)
-    stage = buffers[: count + 1]
-    arrived = buffers[count + 1 : 2 * count + 1]
-    outgoing = buffers[2 * count + 1 : 3 * count + 1]
-    incoming = buffers[3 * count + 1 : 4 * count + 1]
-    late_out, late_in, late_arrived = buffers[4 * count + 1 :]
+    replicas, experts, tensors, chunks, sorts, late, blocks, pairs, rows = sizes
+    widths = chunks + sorts + [late]
+    plain = len(chunks)
+    count = len(widths) - 1
+    raw = buffers[0]
+    arrived = buffers[1 : count + 1]
+    outgoing = buffers[count + 1 : 2 * count + 1]
+    incoming = buffers[2 * count + 1 : 3 * count + 1]
+    staged = buffers[3 * count + 1 : -3]
+    late_out, late_in, late_arrived = buffers[-3:]
     my_replica = lax.axis_index("replica")
     my_expert = lax.axis_index("expert")
     my_tensor = lax.axis_index("tensor")
-    widths = chunks + [late]
     columns = sum(widths)
     starts = [sum(widths[:c]) for c in range(count + 1)]
     groups = [(0, 2), (2, 4), (4, experts)]
 
-    def load(c, d):
+    halves = [(0, 2 * pairs), (2 * pairs, blocks)]
+
+    def load(n, d):
         replica = lax.rem(my_replica + d, replicas)
+        part = pl.ds(0, chunks[0]) if n == 0 else pl.ds(chunks[0], columns - chunks[0])
         return pltpu.make_async_copy(
-            delta.at[:, pl.ds(starts[c], widths[c]), replica],
-            stage[c].at[d - 1],
-            load_sem.at[c, d - 1],
+            delta.at[:, part, replica],
+            raw.at[d - 1, :, part],
+            load_sem.at[n, d - 1],
         )
 
-    def y_copy(c, d):
+    def arrival(c, h):
+        return c + h + max(c - plain, 0)
+
+    def y_copy(c, h, d):
+        low, high = halves[h]
+        if c == count:
+            source, goal = late_in.at[:, d], late_arrived.at[d - 1]
+        elif c < plain:
+            source, goal = raw.at[d - 1, :, pl.ds(starts[c], widths[c])], arrived[c].at[d - 1]
+        else:
+            part = (d - 1, pl.ds(low, high - low))
+            source, goal = staged[c - plain].at[part], arrived[c].at[part]
         return pltpu.make_async_remote_copy(
-            src_ref=late_in.at[:, d] if c == count else stage[c].at[d - 1],
-            dst_ref=late_arrived.at[d - 1] if c == count else arrived[c].at[d - 1],
+            src_ref=source,
+            dst_ref=goal,
             send_sem=y_send,
-            recv_sem=y_recv.at[c],
+            recv_sem=y_recv.at[arrival(c, h)],
             device_id={"replica": lax.rem(my_replica + d, replicas)},
             device_id_type=MESH,
         )
@@ -128,6 +153,17 @@
             device_id_type=MESH,
         )
 
+    def sorted_copy(c, e):
+        d = between(my_expert, e, experts)
+        return pltpu.make_async_remote_copy(
+            src_ref=outgoing[c].at[pl.ds(e * pairs, pairs)],
+            dst_ref=incoming[c].at[pl.ds(d * pairs, pairs)],
+            send_sem=z_send,
+            recv_sem=z_recv.at[c, jnp.minimum(lax.div(d, 2), 2)],
+            device_id={"expert": e},
+            device_id_type=MESH,
+        )
+
     def group_of(d):
         return [g for g, (low, high) in enumerate(groups) if low <= d < high][0]
 
@@ -152,9 +188,9 @@
             pl.semaphore_signal(
                 barrier, inc=1, device_id={axis: lax.rem(mine + d, size)}, device_id_type=MESH
             )
-    for c in range(count + 1):
+    for n in range(2):
         for d in range(1, replicas):
-            load(c, d).start()
+            load(n, d).start()
     index_copies = [
         pltpu.make_async_copy(block_map_far, block_map, index_sem.at[0]),
         pltpu.make_async_copy(step_offsets_far, step_offsets, index_sem.at[1]),
@@ -169,16 +205,15 @@
     def digits(key, k):
         return jnp.maximum(lax.rem(lax.div(key, jnp.int32(blocks ** (pairs - 1 - k))), jnp.int32(blocks)), 0)
 
-    def note_order(d, carry):
-        low = target(my_expert, d, experts) * blocks
-        key = jnp.int32(0)
-        for j in range(blocks):
-            slot = block_map[my_expert * blocks + j] - low
-            owned = jnp.where(slot >= 0, slot, blocks) < blocks
-            key = jnp.where(owned, key * blocks + j, key)
-        for k in range(pairs):
-            order[d * pairs + k] = digits(key, k)
-        return carry
+    def note_order():
+        owners = [lax.div(block_map[my_expert * blocks + j], jnp.int32(blocks)) for j in range(blocks)]
+        for d in range(experts):
+            wanted = target(my_expert, d, experts)
+            key = jnp.int32(0)
+            for j in range(blocks):
+                key = jnp.where(owners[j] == wanted, key * blocks + j, key)
+            for k in range(pairs):
+                order[d * pairs + k] = digits(key, k)
 
     def note_slots(d, carry):
         low = origin(my_expert, d, experts) * blocks
@@ -199,32 +234,54 @@
         return carry
 
     pl.semaphore_wait(barrier, replicas + experts + tensors - 3)
-    early = min(EARLY, count)
-    for c in range(early):
-        for d in range(1, replicas):
-            load(c, d).wait()
-            y_copy(c, d).start()
+    for d in range(1, replicas):
+        load(0, d).wait()
+        y_copy(0, 0, d).start()
 
     for copy in index_copies:
         copy.wait()
-    lax.fori_loop(0, experts, note_order, 0)
+    note_order()
+
+    def block_of(j):
+        return order[between(my_expert, j // pairs, experts) * pairs + j % pairs]
+
+    def gather(c, h):
+        dense = widths[c] * rows
+        far = raw.reshape(replicas - 1, blocks, columns * rows, LANES)
+        goal = staged[c - plain].reshape(replicas - 1, blocks, dense, LANES)
+        for j in range(*halves[h]):
+            for r in range(1, replicas):
+                goal[r - 1, j] = far[r - 1, block_of(j), pl.ds(starts[c] * rows, dense)]
+
+    stream = [(0, 0)] + [(c, 0) for c in range(plain, count)] + [(c, 0) for c in range(1, plain)]
+    for c in range(plain, count):
+        stream.insert(min(REST[c - plain], len(stream)), (c, 1))
+
+    def send(part):
+        for c, h in part:
+            if c >= plain:
+                gather(c, h)
+            for d in range(1, replicas):
+                y_copy(c, h, d).start()
+
+    for d in range(1, replicas):
+        load(1, d).wait()
+    send(stream[1:AHEAD])
 
     own_load.wait()
-    for c in range(early, count + 1):
-        for d in range(1, replicas):
-            load(c, d).wait()
     late_dense = late * rows
     for d in range(experts):
         held = (late_in if d == 0 else late_out).reshape(experts, replicas, pairs, late_dense, LANES)
         own_flat = own.reshape(blocks, columns * rows, LANES)
-        rest = stage[count].reshape(replicas - 1, blocks, late_dense, LANES)
+        rest = raw.reshape(replicas - 1, blocks, columns * rows, LANES)
         for k in range(pairs):
             block = order[d * pairs + k]
             held[d, 0, k] = own_flat[block, pl.ds(starts[count] * rows, late_dense)]
             for r in range(1, replicas):
-                held[d, r, k] = rest[r - 1, block]
+                held[d, r, k] = rest[r - 1, block, pl.ds(starts[count] * rows, late_dense)]
     for d in reversed(range(1, experts)):
         z_copy(count, d).start()
+    send(stream[AHEAD:])
 
     lax.fori_loop(0, experts, note_slots, 0)
     lax.fori_loop(0, blocks, note_places, 0)
@@ -239,18 +296,20 @@
     fix_one = 1.0 - beta_one**outer_round
     fix_two = 1.0 - beta_two**outer_round
 
-    def add_up(c):
-        all_of(arrived[c], y_recv.at[c]).wait()
-        dense = chunks[c] * rows
+    def add_up(c, h):
+        low, high = halves[h] if c >= plain else (0, blocks)
+        got = arrived[c].at[:, pl.ds(low, high - low)]
+        all_of(got, y_recv.at[arrival(c, h)]).wait()
+        dense = widths[c] * rows
         part = pl.ds(starts[c] * rows, dense)
         own_flat = own.reshape(blocks, columns * rows, LANES)
         others = arrived[c].reshape(replicas - 1, blocks, dense, LANES)
         out = outgoing[c].reshape(blocks, dense, LANES)
-        for q in range(blocks):
-            block = order[q]
+        for q in range(low, high):
+            block = block_of(q) if c >= plain else order[q]
             value = own_flat[block, part].astype(jnp.float32) * weights[0]
             for d in range(1, replicas):
-                value = value + others[d - 1, block].astype(jnp.float32) * weights[d]
+                value = value + others[d - 1, q if c >= plain else block].astype(jnp.float32) * weights[d]
             out[q] = value.astype(jnp.bfloat16)
 
     def adam(c, q, gradient):
@@ -265,20 +324,19 @@
         held[q, part] = (state[0, slot, part] - update).astype(jnp.bfloat16)
 
     def finish(c, g):
-        if c == 0 and g == 0:
-            all_of(state, state_sem).wait()
         low, high = groups[g]
         got = (max(low, 1) * pairs, high * pairs)
         all_of(incoming[c].at[pl.ds(got[0], got[1] - got[0])], z_recv.at[c, g]).wait()
-        dense = chunks[c] * rows
+        dense = widths[c] * rows
         for q in range(low * pairs, high * pairs):
             terms = (outgoing[c] if q < pairs else incoming[c]).reshape(blocks, dense, LANES)
-            adam(c, q, terms[q].astype(jnp.float32))
+            place = my_expert * pairs + q if q < pairs and c >= plain else q
+            adam(c, q, terms[place].astype(jnp.float32))
         for d in range(1, tensors):
             x_copy(c, low, high, d).start()
 
     def finish_late():
-        all_of(late_arrived, y_recv.at[count]).wait()
+        all_of(late_arrived, y_recv.at[arrival(count, 0)]).wait()
         mine = late_in.reshape(experts, replicas, pairs, late_dense, LANES)
         others = late_arrived.reshape(replicas - 1, experts, pairs, late_dense, LANES)
         for q in range(blocks):
@@ -301,20 +359,30 @@
             new_second[s, part] = second_held[place, part]
             flat[s, goal] = held[place, part]
 
-    def add_and_send(c):
-        add_up(c)
-        for d in reversed(range(1, experts)):
-            z_copy(c, d).start()
+    def add_and_send(c, h):
+        add_up(c, h)
+        if c < plain:
+            for d in reversed(range(1, experts)):
+                z_copy(c, d).start()
+            return
+        for e in range(halves[h][0] // pairs, halves[h][1] // pairs):
+            pl.when(my_expert != e)(sorted_copy(c, e).start)
 
     def turn():
         all_of(late_in.at[pl.ds(1, experts - 1)], late_recv).wait()
-        for c in [count] + list(range(early, count)):
-            for d in range(1, replicas):
-                y_copy(c, d).start()
-
-    def last(c):
-        finish(c, 2)
-        settle(c)
+        for d in range(1, replicas):
+            y_copy(count, 0, d).start()
+
+    def ready(c, h, g):
+        def act():
+            finish(c, g)
+            if g == 2:
+                settle(c)
+
+        if c < plain:
+            act()
+        else:
+            pl.when(my_expert < 2 if h == 0 else my_expert >= 2)(act)
 
     def whole_late():
         finish_late()
@@ -322,15 +390,14 @@
 
     steps = [(TURN, 0, turn)]
     landed = 0
-    for c in list(range(early)) + [count] + list(range(early, count)):
-        landed += widths[c]
-        if c == count:
-            steps.append((landed, 2, whole_late))
-            continue
-        steps.append((landed, 1, functools.partial(add_and_send, c)))
-        steps.append((landed + LAGS[0], 3, functools.partial(finish, c, 0)))
-        steps.append((landed + LAGS[1], 4, functools.partial(finish, c, 1)))
-        steps.append((landed + LAGS[2], 5, functools.partial(last, c)))
+    for c, h in stream:
+        landed += widths[c] * (halves[h][1] - halves[h][0]) // blocks if c >= plain else widths[c]
+        steps.append((landed, 1, functools.partial(add_and_send, c, h)))
+        for g in range(3):
+            lag = FIRST_LAGS[g] if c >= plain and h == 0 else LAGS[g]
+            steps.append((landed + lag, 3 + g, functools.partial(ready, c, h, g)))
+    steps.append((landed + late, 2, whole_late))
+    all_of(state, state_sem).wait()
     for _, _, step in sorted(steps, key=lambda entry: entry[:2]):
         step()
 
@@ -364,9 +431,8 @@
 
 
 def split(columns):
-    late = LATE
-    middle = columns - late - 2 * EDGE
-    return [EDGE] + [CHUNK] * (middle // CHUNK) + [EDGE] * (1 + middle % CHUNK // EDGE), late
+    middle = columns - LATE - sum(SORTS) - EDGE
+    return [EDGE] + [CHUNK] * (middle // CHUNK), list(SORTS), LATE
 
 
 def body(delta, step_offsets, block_map, master_params, first_moment, second_moment, *, shape):
@@ -375,8 +441,9 @@
     rows = rows_all // replicas
     columns = width // LANES
     pairs = blocks // experts
-    chunks, late = split(columns)
-    count = len(chunks)
+    chunks, sorts, late = split(columns)
+    widths = chunks + sorts
+    count = len(widths)
     terms = delta.reshape(blocks, replicas, rows, columns, LANES).transpose(0, 3, 1, 2, 4)
 
     def dense(state):
@@ -392,7 +459,7 @@
     anywhere = pl.BlockSpec(memory_space=pltpu.HBM)
     near = pl.BlockSpec(memory_space=pltpu.VMEM)
     dma = pltpu.SemaphoreType.DMA
-    sizes = (replicas, experts, tensors, chunks, late, blocks, pairs, rows)
+    sizes = (replicas, experts, tensors, chunks, sorts, late, blocks, pairs, rows)
     piece = (rows, LANES)
     held = pl.pallas_call(
         functools.partial(kernel, sizes),
@@ -416,21 +483,21 @@
             pltpu.SMEM((blocks,), jnp.int32),
             pltpu.SMEM((blocks,), jnp.int32),
             dma((2,)),
-            dma((count + 1, replicas - 1)),
-            dma,
-            dma,
-            dma,
-            dma((count + 1,)),
+            dma((2, replicas - 1)),
+            dma,
+            dma,
+            dma,
+            dma((count + len(sorts) + 1,)),
             dma,
             dma((count, 3)),
             dma,
             dma,
             dma,
         ]
-        + [pltpu.VMEM((replicas - 1, blocks, c) + piece, jnp.bfloat16) for c in chunks + [late]]
-        + [pltpu.VMEM((replicas - 1, blocks, c) + piece, jnp.bfloat16) for c in chunks]
-        + [pltpu.VMEM((blocks, c) + piece, jnp.bfloat16) for c in chunks]
-        + [pltpu.VMEM((blocks, c) + piece, jnp.bfloat16) for c in chunks]
+        + [pltpu.VMEM((replicas - 1, blocks, columns) + piece, jnp.bfloat16)]
+        + [pltpu.VMEM((replicas - 1, blocks, c) + piece, jnp.bfloat16) for c in widths]
+        + [pltpu.VMEM((blocks, c) + piece, jnp.bfloat16) for c in widths] * 2
+        + [pltpu.VMEM((replicas - 1, blocks, c) + piece, jnp.bfloat16) for c in sorts]
         + [pltpu.VMEM((experts, replicas, pairs, late) + piece, jnp.bfloat16)] * 2
         + [pltpu.VMEM((replicas - 1, experts, pairs, late) + piece, jnp.bfloat16)],
         compiler_params=pltpu.CompilerParams(collective_id=0, has_side_effects=True),

time: 27.5 us -> 26.6 us (0.967)
  Pallas kernels: 26.8 us -> 25.8 us
    pallas_call x1, Pallas kernels: 25.2 us -> 24.2 us  [body(): pl.pallas_call(functools.partial(kernel, sizes), out_shape=(pltpu.VMEM(pa...]
where the time goes in v3:
time: 26.6 us; the launch traced here: 26.4 us
  Pallas kernels  25.8 us (97%)
  between operations  0.64 us (2%)
    pallas_call x1, Pallas kernels, body(): pl.pallas_call(functools.partial(kernel, sizes), out_shape=(pltpu.VMEM(pa...  24.2 us
    pallas_call x1, Pallas kernels, body(): pl.pallas_call(write_out, out_shape=(jax.ShapeDtypeStruct(params_shape, j...  1.56 us

profile of v3, /device:TPU:0, one launch (start us, length us, event | category | flops | bytes accessed | tf_op | source)
XLA Modules:
  0.0 26.4 jit_solution(10267145415182852926)
XLA Ops:
  0.6 24.2 %shard_map.85 = (bf16[16,112,2,128]{3,2,1,0:T(2,128)(2,1)S(1)}, f32[16,112,128]{2,1,0:T(8,128)S(1)}, f32[16,112,128]{2,1,0:T(8,128)S(1)}) custom-call(s32[128]{0:T(128)} %block_map_far.1, s32[2]{0:T(128)} %step_offsets_far.1, bf16[16,56,2,2,128]{4,3,2,1,0:T(2,128)(2,1)} %bitcast.31, f32[16,112,128]{2,1,0:T(8,128)} %bitcast.32, f32[16,112,128]{2,1,0:T(8,128)} %bitcast.33, ...), custom_call_target="tpu_custom_call" | custom-call | tf_op jit(solution)/shard_map/pallas_call | solution.py:464
  24.9 1.6 %shard_map.86 = (bf16[16,112,2,128]{3,2,1,0:T(2,128)(2,1)}, f32[16,112,128]{2,1,0:T(8,128)}, f32[16,112,128]{2,1,0:T(8,128)}) custom-call(bf16[16,112,2,128]{3,2,1,0:T(2,128)(2,1)S(1)} %get-tuple-element.9.refs_0_, f32[16,112,128]{2,1,0:T(8,128)S(1)} %get-tuple-element.10.refs_1_, f32[16,112,128]{2,1,0:T(8,128)S(1)} %get-tuple-element.11.refs_2_), custom_call_target="tpu_custom_call" | custom-call | tf_op jit(solution)/shard_map/pallas_call | solution.py:505

commit v4 on v3

--- a/solution.py
+++ b/solution.py
@@ -15,14 +15,11 @@
 
 LANES = 128
 CHUNK = 4
-EDGE = 4
 LATE = 8
 SORTS = (4, 4)
-REST = (11, 13)
 AHEAD = 7
 TURN = 21
 LAGS = (8, 16, 24)
-FIRST_LAGS = (8, 16, 24)
 MESH = pl.DeviceIdType.MESH
 
 
@@ -97,27 +94,30 @@
     widths = chunks + sorts + [late]
     plain = len(chunks)
     count = len(widths) - 1
-    raw = buffers[0]
-    arrived = buffers[1 : count + 1]
-    outgoing = buffers[count + 1 : 2 * count + 1]
-    incoming = buffers[2 * count + 1 : 3 * count + 1]
-    staged = buffers[3 * count + 1 : -3]
+    raw = buffers[:2]
+    arrived = buffers[2 : count + 2]
+    outgoing = buffers[count + 2 : 2 * count + 2]
+    incoming = buffers[2 * count + 2 : 3 * count + 2]
+    staged = buffers[3 * count + 2 : -3]
     late_out, late_in, late_arrived = buffers[-3:]
     my_replica = lax.axis_index("replica")
     my_expert = lax.axis_index("expert")
     my_tensor = lax.axis_index("tensor")
     columns = sum(widths)
-    starts = [sum(widths[:c]) for c in range(count + 1)]
+    head = sum(sorts)
+    edge = head + chunks[0]
+    starts = [head + sum(widths[:c]) for c in range(plain)]
+    starts += [sum(sorts[:c]) for c in range(count - plain)] + [columns - late]
     groups = [(0, 2), (2, 4), (4, experts)]
 
     halves = [(0, 2 * pairs), (2 * pairs, blocks)]
 
     def load(n, d):
         replica = lax.rem(my_replica + d, replicas)
-        part = pl.ds(0, chunks[0]) if n == 0 else pl.ds(chunks[0], columns - chunks[0])
+        part = pl.ds(0, edge) if n == 0 else pl.ds(edge, columns - edge)
         return pltpu.make_async_copy(
             delta.at[:, part, replica],
-            raw.at[d - 1, :, part],
+            raw[n].at[d - 1],
             load_sem.at[n, d - 1],
         )
 
@@ -129,7 +129,8 @@
         if c == count:
             source, goal = late_in.at[:, d], late_arrived.at[d - 1]
         elif c < plain:
-            source, goal = raw.at[d - 1, :, pl.ds(starts[c], widths[c])], arrived[c].at[d - 1]
+            part = pl.ds(starts[c] - edge if c else head, widths[c])
+            source, goal = raw[min(c, 1)].at[d - 1, :, part], arrived[c].at[d - 1]
         else:
             part = (d - 1, pl.ds(low, high - low))
             source, goal = staged[c - plain].at[part], arrived[c].at[part]
@@ -188,15 +189,15 @@
             pl.semaphore_signal(
                 barrier, inc=1, device_id={axis: lax.rem(mine + d, size)}, device_id_type=MESH
             )
-    for n in range(2):
-        for d in range(1, replicas):
-            load(n, d).start()
     index_copies = [
         pltpu.make_async_copy(block_map_far, block_map, index_sem.at[0]),
         pltpu.make_async_copy(step_offsets_far, step_offsets, index_sem.at[1]),
     ]
     for copy in index_copies:
         copy.start()
+    for n in range(2):
+        for d in range(1, replicas):
+            load(n, d).start()
     own_load = pltpu.make_async_copy(delta.at[:, :, my_replica], own, own_sem)
     own_load.start()
     for i, source in enumerate((master_params, first_moment, second_moment)):
@@ -233,29 +234,23 @@
         places[s] = place
         return carry
 
-    pl.semaphore_wait(barrier, replicas + experts + tensors - 3)
-    for d in range(1, replicas):
-        load(0, d).wait()
-        y_copy(0, 0, d).start()
-
     for copy in index_copies:
         copy.wait()
     note_order()
-
+    pl.semaphore_wait(barrier, replicas + experts + tensors - 3)
     def block_of(j):
         return order[between(my_expert, j // pairs, experts) * pairs + j % pairs]
 
     def gather(c, h):
         dense = widths[c] * rows
-        far = raw.reshape(replicas - 1, blocks, columns * rows, LANES)
+        far = raw[0].reshape(replicas - 1, blocks, edge * rows, LANES)
         goal = staged[c - plain].reshape(replicas - 1, blocks, dense, LANES)
         for j in range(*halves[h]):
             for r in range(1, replicas):
                 goal[r - 1, j] = far[r - 1, block_of(j), pl.ds(starts[c] * rows, dense)]
 
-    stream = [(0, 0)] + [(c, 0) for c in range(plain, count)] + [(c, 0) for c in range(1, plain)]
-    for c in range(plain, count):
-        stream.insert(min(REST[c - plain], len(stream)), (c, 1))
+    stream = [(c, 0) for c in range(plain, count)] + [(c, 0) for c in range(plain)]
+    stream += [(c, 1) for c in range(plain, count)]
 
     def send(part):
         for c, h in part:
@@ -265,20 +260,24 @@
                 y_copy(c, h, d).start()
 
     for d in range(1, replicas):
+        load(0, d).wait()
+    first = count - plain + 1
+    send(stream[:first])
+    for d in range(1, replicas):
         load(1, d).wait()
-    send(stream[1:AHEAD])
+    send(stream[first:AHEAD])
 
     own_load.wait()
     late_dense = late * rows
     for d in range(experts):
         held = (late_in if d == 0 else late_out).reshape(experts, replicas, pairs, late_dense, LANES)
         own_flat = own.reshape(blocks, columns * rows, LANES)
-        rest = raw.reshape(replicas - 1, blocks, columns * rows, LANES)
+        rest = raw[1].reshape(replicas - 1, blocks, (columns - edge) * rows, LANES)
         for k in range(pairs):
             block = order[d * pairs + k]
             held[d, 0, k] = own_flat[block, pl.ds(starts[count] * rows, late_dense)]
             for r in range(1, replicas):
-                held[d, r, k] = rest[r - 1, block, pl.ds(starts[count] * rows, late_dense)]
+                held[d, r, k] = rest[r - 1, block, pl.ds((starts[count] - edge) * rows, late_dense)]
     for d in reversed(range(1, experts)):
         z_copy(count, d).start()
     send(stream[AHEAD:])
@@ -394,8 +393,7 @@
         landed += widths[c] * (halves[h][1] - halves[h][0]) // blocks if c >= plain else widths[c]
         steps.append((landed, 1, functools.partial(add_and_send, c, h)))
         for g in range(3):
-            lag = FIRST_LAGS[g] if c >= plain and h == 0 else LAGS[g]
-            steps.append((landed + lag, 3 + g, functools.partial(ready, c, h, g)))
+            steps.append((landed + LAGS[g], 3 + g, functools.partial(ready, c, h, g)))
     steps.append((landed + late, 2, whole_late))
     all_of(state, state_sem).wait()
     for _, _, step in sorted(steps, key=lambda entry: entry[:2]):
@@ -431,8 +429,8 @@
 
 
 def split(columns):
-    middle = columns - LATE - sum(SORTS) - EDGE
-    return [EDGE] + [CHUNK] * (middle // CHUNK), list(SORTS), LATE
+    middle = columns - LATE - sum(SORTS)
+    return [CHUNK] * (middle // CHUNK), list(SORTS), LATE
 
 
 def body(delta, step_offsets, block_map, master_params, first_moment, second_moment, *, shape):
@@ -444,6 +442,7 @@
     chunks, sorts, late = split(columns)
     widths = chunks + sorts
     count = len(widths)
+    edge = sum(sorts) + chunks[0]
     terms = delta.reshape(blocks, replicas, rows, columns, LANES).transpose(0, 3, 1, 2, 4)
 
     def dense(state):
@@ -494,7 +493,7 @@
             dma,
             dma,
         ]
-        + [pltpu.VMEM((replicas - 1, blocks, columns) + piece, jnp.bfloat16)]
+        + [pltpu.VMEM((replicas - 1, blocks, c) + piece, jnp.bfloat16) for c in (edge, columns - edge)]
         + [pltpu.VMEM((replicas - 1, blocks, c) + piece, jnp.bfloat16) for c in widths]
         + [pltpu.VMEM((blocks, c) + piece, jnp.bfloat16) for c in widths] * 2
         + [pltpu.VMEM((replicas - 1, blocks, c) + piece, jnp.bfloat16) for c in sorts]

time: 26.6 us -> 26.4 us (level)
  no operation moved by 1% of the time
where the time goes in v4:
time: 26.4 us; the launch traced here: 26.3 us
  Pallas kernels  25.6 us (97%)
  between operations  0.64 us (2%)
    pallas_call x1, Pallas kernels, body(): pl.pallas_call(functools.partial(kernel, sizes), out_shape=(pltpu.VMEM(pa...  24.1 us
    pallas_call x1, Pallas kernels, body(): pl.pallas_call(write_out, out_shape=(jax.ShapeDtypeStruct(params_shape, j...  1.56 us

profile of v4, /device:TPU:0, one launch (start us, length us, event | category | flops | bytes accessed | tf_op | source)
XLA Modules:
  0.0 26.3 jit_solution(12871113134097859737)
XLA Ops:
  0.6 24.1 %shard_map.85 = (bf16[16,112,2,128]{3,2,1,0:T(2,128)(2,1)S(1)}, f32[16,112,128]{2,1,0:T(8,128)S(1)}, f32[16,112,128]{2,1,0:T(8,128)S(1)}) custom-call(s32[128]{0:T(128)} %block_map_far.1, s32[2]{0:T(128)} %step_offsets_far.1, bf16[16,56,2,2,128]{4,3,2,1,0:T(2,128)(2,1)} %bitcast.31, f32[16,112,128]{2,1,0:T(8,128)} %bitcast.32, f32[16,112,128]{2,1,0:T(8,128)} %bitcast.33, ...), custom_call_target="tpu_custom_call" | custom-call | tf_op jit(solution)/shard_map/pallas_call | solution.py:463
  24.7 1.6 %shard_map.86 = (bf16[16,112,2,128]{3,2,1,0:T(2,128)(2,1)}, f32[16,112,128]{2,1,0:T(8,128)}, f32[16,112,128]{2,1,0:T(8,128)}) custom-call(bf16[16,112,2,128]{3,2,1,0:T(2,128)(2,1)S(1)} %get-tuple-element.9.refs_0_, f32[16,112,128]{2,1,0:T(8,128)S(1)} %get-tuple-element.10.refs_1_, f32[16,112,128]{2,1,0:T(8,128)S(1)} %get-tuple-element.11.refs_2_), custom_call_target="tpu_custom_call" | custom-call | tf_op jit(solution)/shard_map/pallas_call | solution.py:504

commit v5 on v4

--- a/solution.py
+++ b/solution.py
@@ -16,7 +16,7 @@
 LANES = 128
 CHUNK = 4
 LATE = 8
-SORTS = (4, 4)
+SORTS = (4, 4, 4)
 AHEAD = 7
 TURN = 21
 LAGS = (8, 16, 24)

time: 26.4 us -> 26.2 us (level)
  Pallas kernels: 25.6 us -> 25.3 us
    pallas_call x1, Pallas kernels: 24.1 us -> 23.7 us  [body(): pl.pallas_call(functools.partial(kernel, sizes), out_shape=(pltpu.VMEM(pa...]
where the time goes in v5:
time: 26.2 us; the launch traced here: 25.9 us
  Pallas kernels  25.3 us (97%)
  between operations  0.64 us (2%)
    pallas_call x1, Pallas kernels, body(): pl.pallas_call(functools.partial(kernel, sizes), out_shape=(pltpu.VMEM(pa...  23.7 us
    pallas_call x1, Pallas kernels, body(): pl.pallas_call(write_out, out_shape=(jax.ShapeDtypeStruct(params_shape, j...  1.56 us

profile of v5, /device:TPU:0, one launch (start us, length us, event | category | flops | bytes accessed | tf_op | source)
XLA Modules:
  0.0 25.9 jit_solution(1845962643042287374)
XLA Ops:
  0.6 23.7 %shard_map.85 = (bf16[16,112,2,128]{3,2,1,0:T(2,128)(2,1)S(1)}, f32[16,112,128]{2,1,0:T(8,128)S(1)}, f32[16,112,128]{2,1,0:T(8,128)S(1)}) custom-call(s32[128]{0:T(128)} %block_map_far.1, s32[2]{0:T(128)} %step_offsets_far.1, bf16[16,56,2,2,128]{4,3,2,1,0:T(2,128)(2,1)} %bitcast.31, f32[16,112,128]{2,1,0:T(8,128)} %bitcast.32, f32[16,112,128]{2,1,0:T(8,128)} %bitcast.33, ...), custom_call_target="tpu_custom_call" | custom-call | tf_op jit(solution)/shard_map/pallas_call | solution.py:463
  24.4 1.6 %shard_map.86 = (bf16[16,112,2,128]{3,2,1,0:T(2,128)(2,1)}, f32[16,112,128]{2,1,0:T(8,128)}, f32[16,112,128]{2,1,0:T(8,128)}) custom-call(bf16[16,112,2,128]{3,2,1,0:T(2,128)(2,1)S(1)} %get-tuple-element.9.refs_0_, f32[16,112,128]{2,1,0:T(8,128)S(1)} %get-tuple-element.10.refs_1_, f32[16,112,128]{2,1,0:T(8,128)S(1)} %get-tuple-element.11.refs_2_), custom_call_target="tpu_custom_call" | custom-call | tf_op jit(solution)/shard_map/pallas_call | solution.py:504

commit v6 on v5

--- a/solution.py
+++ b/solution.py
@@ -19,7 +19,7 @@
 SORTS = (4, 4, 4)
 AHEAD = 7
 TURN = 21
-LAGS = (8, 16, 24)
+LAGS = (8, 16, 23)
 MESH = pl.DeviceIdType.MESH
 
 

time: 26.2 us -> 26.1 us (level)
  no operation moved by 1% of the time
where the time goes in v6:
time: 26.1 us; the launch traced here: 25.9 us
  Pallas kernels  25.3 us (97%)
  between operations  0.64 us (2%)
    pallas_call x1, Pallas kernels, body(): pl.pallas_call(functools.partial(kernel, sizes), out_shape=(pltpu.VMEM(pa...  23.7 us
    pallas_call x1, Pallas kernels, body(): pl.pallas_call(write_out, out_shape=(jax.ShapeDtypeStruct(params_shape, j...  1.56 us

profile of v6, /device:TPU:0, one launch (start us, length us, event | category | flops | bytes accessed | tf_op | source)
XLA Modules:
  0.0 25.9 jit_solution(16283498739382134226)
XLA Ops:
  0.6 23.7 %shard_map.85 = (bf16[16,112,2,128]{3,2,1,0:T(2,128)(2,1)S(1)}, f32[16,112,128]{2,1,0:T(8,128)S(1)}, f32[16,112,128]{2,1,0:T(8,128)S(1)}) custom-call(s32[128]{0:T(128)} %block_map_far.1, s32[2]{0:T(128)} %step_offsets_far.1, bf16[16,56,2,2,128]{4,3,2,1,0:T(2,128)(2,1)} %bitcast.31, f32[16,112,128]{2,1,0:T(8,128)} %bitcast.32, f32[16,112,128]{2,1,0:T(8,128)} %bitcast.33, ...), custom_call_target="tpu_custom_call" | custom-call | tf_op jit(solution)/shard_map/pallas_call | solution.py:463
  24.4 1.6 %shard_map.86 = (bf16[16,112,2,128]{3,2,1,0:T(2,128)(2,1)}, f32[16,112,128]{2,1,0:T(8,128)}, f32[16,112,128]{2,1,0:T(8,128)}) custom-call(bf16[16,112,2,128]{3,2,1,0:T(2,128)(2,1)S(1)} %get-tuple-element.9.refs_0_, f32[16,112,128]{2,1,0:T(8,128)S(1)} %get-tuple-element.10.refs_1_, f32[16,112,128]{2,1,0:T(8,128)S(1)} %get-tuple-element.11.refs_2_), custom_call_target="tpu_custom_call" | custom-call | tf_op jit(solution)/shard_map/pallas_call | solution.py:504
